TPU v7x, 128 devices: a whole 4x4x4 slice. The times are simulated.
128 devices in a mesh: section: 4 (over x), dp: 32 (over y, z, core).
Axes of the slice: x: 4, y: 4, z: 4, core: 2. Of those that a mesh axis runs over, the one named last changes fastest.
Arguments:
- clip_pool: bfloat16 [1024, 256, 512], P('dp'), may hold values from -8 to 8
- clip_index: int32 [8, 128], P(None, 'dp'), may hold values from 0 to 31, as said below
- batch_order: int32 [8], replicated, may hold values from 0 to 7, each once
- tap_weights: bfloat16 [4, 3, 512, 512], P('section'), may hold values from -0.15625 to 0.15625
- out_weights: bfloat16 [4, 512, 512], P('section'), may hold values from -0.25 to 0.25
- norm_gains: bfloat16 [4, 512], P('section'), may hold values from 0.099609375 to 1.8984375
- quant_weight: bfloat16 [512, 18], replicated, may hold values from -0.25 to 0.25
- quant_bias: float32 [18], replicated, may hold values from -3 to 3
- post_weight: bfloat16 [18, 512], replicated, may hold values from -1.5 to 1.5
Outputs:
- row_error: float32 [8, 128, 256], P('section', 'dp')
- entropy_loss: float32 [8], replicated
Inputs may be any that keep to these rules, and one draw needn't show every extreme that they name: `clip_index`: entries index the clips of the replica that holds the column; over all 8 micro-batches, the 4 columns of one replica name each of its 32 clips exactly once. `batch_order`: each micro-batch number 0 to 7 once.
All inputs are finite; a program needn't handle non-finite values.
Results may differ from a plain program's by a relative error of at most 0.0015.
Values may be sent and summed in bfloat16 or wider, within the bound.
A program may use at most 128 MiB of HBM per device.

v0:
```python
import functools

import jax
import jax.numpy as jnp
from jax import lax
from jax.sharding import Mesh
from jax.sharding import PartitionSpec as P

SPATIAL = 64
DP = ("dp_0", "dp_1", "dp_2")
SECTION_DP = ("section", "dp_0", "dp_1", "dp_2")


norm_eps = 1e-06
quant_section = 1


def over_axes(array, axes):
    return functools.reduce(lax.psum, axes, array)


def run_block(current, tap_set, out_weight, gain_row):
    clip_count, row_count, channels = current.shape
    widened = current.astype(jnp.float32)
    scale = lax.rsqrt(jnp.mean(widened * widened, axis=-1, keepdims=True) + norm_eps)
    normed = (widened * scale * gain_row.astype(jnp.float32)).astype(jnp.bfloat16)
    flat = normed.reshape(-1, channels)
    mixed = jnp.zeros((clip_count, row_count, channels), jnp.float32)
    for k in range(tap_set.shape[0]):
        product = jnp.dot(flat, tap_set[k], preferred_element_type=jnp.float32).reshape(
            clip_count, row_count, channels
        )
        moved = jnp.pad(product, ((0, 0), (k * SPATIAL, 0), (0, 0)))[:, :row_count]
        mixed = mixed + moved
    activated = jax.nn.silu(mixed).astype(jnp.bfloat16)
    update = jnp.dot(
        activated.reshape(-1, channels), out_weight, preferred_element_type=jnp.float32
    )
    return (widened + update.reshape(clip_count, row_count, channels)).astype(jnp.bfloat16)


def quantize(current, quant_weight, quant_bias, post_weight):
    channels = current.shape[-1]
    logits = (
        jnp.dot(current.reshape(-1, channels), quant_weight, preferred_element_type=jnp.float32)
        + quant_bias
    )
    bit_prob = jax.nn.sigmoid(4.0 * logits)
    codes = (2.0 * bit_prob - 1.0).astype(jnp.bfloat16)
    quantized = jnp.dot(codes, post_weight, preferred_element_type=jnp.float32).astype(jnp.bfloat16)
    bit_sums = jnp.sum(bit_prob, axis=0)
    entropy_sum = -jnp.sum(
        bit_prob * jax.nn.log_sigmoid(4.0 * logits)
        + (1.0 - bit_prob) * jax.nn.log_sigmoid(-4.0 * logits)
    )
    return (quantized.reshape(current.shape), bit_sums, entropy_sum)


def squared_error(decoded, source):
    differ = decoded.astype(jnp.float32) - source.astype(jnp.float32)
    return jnp.mean(differ * differ, axis=-1)


def final_entropy(bit_buffer, entropy_buffer, batch_order, rows_total):
    marginal = bit_buffer / rows_total
    sample_entropy = entropy_buffer / rows_total
    averaged = jnp.zeros_like(marginal)
    running = marginal[batch_order[0]]
    for t in range(batch_order.shape[0]):
        if t > 0:
            running = 0.5 * running + 0.5 * marginal[batch_order[t]]
        averaged = averaged.at[batch_order[t]].set(running)
    smoothed = 0.05 + 0.9 * averaged
    code_entropy = -jnp.sum(
        smoothed * jnp.log(smoothed) + (1.0 - smoothed) * jnp.log(1.0 - smoothed), axis=-1
    )
    return sample_entropy - code_entropy


def on_device(
    clip_pool,
    clip_index,
    batch_order,
    tap_weights,
    out_weights,
    norm_gains,
    quant_weight,
    quant_bias,
    post_weight,
):
    section_id = lax.axis_index("section")
    sections = lax.axis_size("section")
    batches = batch_order.shape[0]
    clip_count = clip_index.shape[1]
    row_count = clip_pool.shape[1]
    rows_total = float(clip_count * lax.axis_size(DP) * row_count)
    bit_buffer = jnp.zeros((batches, quant_weight.shape[1]), jnp.float32)
    entropy_buffer = jnp.zeros((batches,), jnp.float32)
    all_taps, all_out, all_gains = (
        lax.all_gather(tap_weights, "section", axis=0, tiled=True),
        lax.all_gather(out_weights, "section", axis=0, tiled=True),
        lax.all_gather(norm_gains, "section", axis=0, tiled=True),
    )
    per_section = batches // sections
    error_list = []
    for i in range(per_section):
        batch_slot = section_id * per_section + i
        source = jnp.take(clip_pool, clip_index[batch_slot], axis=0)
        current = source
        for s in range(sections):
            current = run_block(current, all_taps[s], all_out[s], all_gains[s])
            if s == quant_section:
                current, bit_sums, entropy_sum = quantize(
                    current, quant_weight, quant_bias, post_weight
                )
                bit_buffer = bit_buffer.at[batch_slot].add(bit_sums)
                entropy_buffer = entropy_buffer.at[batch_slot].add(entropy_sum)
        error_list.append(squared_error(current, source))
    bit_buffer, entropy_buffer = (
        over_axes(bit_buffer, SECTION_DP),
        over_axes(entropy_buffer, SECTION_DP),
    )
    error_out = jnp.stack(error_list)
    losses = final_entropy(bit_buffer, entropy_buffer, batch_order, rows_total)
    return (error_out, losses)


def solution(mesh):
    torus = Mesh(
        mesh.devices.reshape(mesh.shape["section"], 4, 4, 2), ("section", "dp_0", "dp_1", "dp_2")
    )
    return jax.shard_map(
        on_device,
        mesh=torus,
        in_specs=(
            P(DP, None, None),
            P(None, DP),
            P(),
            P("section", None, None, None),
            P("section", None, None),
            P("section", None),
            P(),
            P(),
            P(),
        ),
        out_specs=(P("section", DP, None), P()),
        check_vma=False,
    )
```

profile of v0, /device:TPU:1, one launch (start us, length us, event | category | flops | bytes accessed | tf_op | source)
XLA Modules:
  0.0 248.7 jit_solution(16837074438808056096)
XLA Ops:
  7.2 0.7 all-gather.4.cloned.1.call-update
  8.0 0.7 all-gather.6.cloned.1.call-update
  8.7 0.7 fusion.181
  20.1 4.7 %gather_fusion = bf16[4,256,512]{2,1,0:T(8,128)(2,1)S(1)} fusion(bf16[32,256,512]{2,1,0:T(8,128)(2,1)} %param.35, s32[1024]{0:T(1024)S(1)} %pad_clamp_fusion.1), kind=kCustom, calls=%fused_computation.clone | custom fusion | bytes 2097168 | tf_op jit(solution)/shard_map/jit(_take)/gather | solution.py:108
  24.8 4.8 %gather_fusion.1 = bf16[4,256,512]{2,1,0:T(8,128)(2,1)S(1)} fusion(bf16[32,256,512]{2,1,0:T(8,128)(2,1)} %param.35, s32[1024]{0:T(1024)S(1)} %pad_clamp_fusion), kind=kCustom, calls=%fused_computation.1.clone | custom fusion | bytes 2097168 | tf_op jit(solution)/shard_map/jit(_take)/gather | solution.py:108
  34.9 10.8 %all-gather = bf16[4,1,512]{2,1,0:T(2,128)(2,1)S(1)} all-gather(bf16[1,1,512]{2,1,0:T(2,128)(2,1)S(1)} %bitcast.176), channel_id=1, replica_groups=mesh['section'=4,'dp_0'=4,'dp_1'=4,'dp_2'=2] {'section'}, dimensions={0}, use_global_device_ids=true | all-gather | bytes 5120 | tf_op jit(solution)/shard_map/all_gather | solution.py:102
  45.7 0.8 and_reduce_fusion.4
  46.5 0.9 and_reduce_fusion
  48.2 30.2 %all-gather.4.cloned.1.call-done = bf16[4,3,512,512]{3,2,1,0:T(8,128)(2,1)} async-done(((bf16[1,3,512,512]{3,2,1,0:T(8,128)(2,1)}), bf16[4,3,512,512]{3,2,1,0:T(8,128)(2,1)}) %all-gather.4.cloned.1.call-update) | async-done | bytes 6291472 | tf_op jit(solution)/shard_map/all_gather | solution.py:100
  78.5 3.1 %fusion.60 = f32[4,256,512]{2,1,0:T(8,128)} fusion(f32[4,256]{1,0:T(4,128)S(1)} %add_rsqrt_fusion.3, f32[512]{0:T(512)S(1)} %bitcast.189, bf16[4,3,512,512]{3,2,1,0:T(8,128)(2,1)} %all-gather.4.cloned.1.call-done, bf16[4,256,512]{2,1,0:T(8,128)(2,1)S(1)} %gather_fusion.1, pred[4]{0:T(512)(128)(4,1)S(1)} %get-tuple-element.209), kind=kOutput, calls=%fused_computation.107 | convolution fusion | flops 539492352 | bytes 3676164 | tf_op jit(solution)/shard_map/dot_general | solution.py:30
  81.6 3.2 %fusion.58 = f32[4,256,512]{2,1,0:T(8,128)} fusion(f32[4,256]{1,0:T(4,128)S(1)} %add_rsqrt_fusion.3, f32[512]{0:T(512)S(1)} %bitcast.190, bf16[4,3,512,512]{3,2,1,0:T(8,128)(2,1)} %all-gather.4.cloned.1.call-done, bf16[4,256,512]{2,1,0:T(8,128)(2,1)S(1)} %gather_fusion.1, pred[4]{0:T(512)(128)(4,1)S(1)} %get-tuple-element.209), kind=kOutput, calls=%fused_computation.106 | convolution fusion | flops 539492352 | bytes 3676164 | tf_op jit(solution)/shard_map/dot_general | solution.py:30
  84.8 26.6 %all-gather.6.cloned.1.call-done = bf16[4,512,512]{2,1,0:T(8,128)(2,1)} async-done(((bf16[1,512,512]{2,1,0:T(8,128)(2,1)}), bf16[4,512,512]{2,1,0:T(8,128)(2,1)}) %all-gather.6.cloned.1.call-update) | async-done | bytes 2097168 | tf_op jit(solution)/shard_map/all_gather | solution.py:101
  111.4 4.6 %fusion.24 = (f32[4,256]{1,0:T(4,128)S(1)}, bf16[4,256,512]{2,1,0:T(8,128)(2,1)}) fusion(bf16[4,512,512]{2,1,0:T(8,128)(2,1)} %all-gather.6.cloned.1.call-done, f32[4,256,512]{2,1,0:T(8,128)} %fusion.58, f32[4,256,512]{2,1,0:T(8,128)} %fusion.60, f32[4,256]{1,0:T(4,128)S(1)} %add_rsqrt_fusion.3, f32[512]{0:T(512)S(1)} %bitcast.191, ...), kind=kOutput, calls=%fused_computation.62 | convolution fusion | flops 1083702272 | bytes 8399872 | tf_op jit(solution)/shard_map/dot_general | solution.py:36
  116.1 3.5 %fusion.54 = f32[4,256,512]{2,1,0:T(8,128)} fusion(bf16[4,256,512]{2,1,0:T(8,128)(2,1)} %get-tuple-element.194, f32[4,256]{1,0:T(4,128)S(1)} %add_rsqrt_fusion.2, f32[512]{0:T(512)S(1)} %bitcast.183, bf16[4,3,512,512]{3,2,1,0:T(8,128)(2,1)} %all-gather.4.cloned.1.call-done), kind=kOutput, calls=%fused_computation.105 | convolution fusion | flops 538968064 | bytes 3676160 | tf_op jit(solution)/shard_map/dot_general | solution.py:30
  119.6 3.2 %fusion.52 = f32[4,256,512]{2,1,0:T(8,128)} fusion(bf16[4,256,512]{2,1,0:T(8,128)(2,1)S(1)} %copy-done.16, f32[4,256]{1,0:T(4,128)S(1)} %add_rsqrt_fusion.2, f32[512]{0:T(512)S(1)} %bitcast.184, bf16[4,3,512,512]{3,2,1,0:T(8,128)(2,1)} %all-gather.4.cloned.1.call-done), kind=kOutput, calls=%fused_computation.104 | convolution fusion | flops 538968064 | bytes 3676160 | tf_op jit(solution)/shard_map/dot_general | solution.py:30
  122.8 5.2 %fusion.27 = bf16[4,256,512]{2,1,0:T(8,128)(2,1)} fusion(bf16[4,256,512]{2,1,0:T(8,128)(2,1)} %get-tuple-element.194, f32[4,256,512]{2,1,0:T(8,128)} %fusion.52, f32[4,256,512]{2,1,0:T(8,128)} %fusion.54, f32[4,256]{1,0:T(4,128)S(1)} %add_rsqrt_fusion.2, f32[512]{0:T(512)S(1)} %bitcast.185, bf16[4,3,512,512]{3,2,1,0:T(8,128)(2,1)} %all-gather.4.cloned.1.call-done, ...), kind=kOutput, calls=%fused_computation.65 | convolution fusion | flops 1081081856 | bytes 8394752 | tf_op jit(solution)/shard_map/dot_general | solution.py:36
  128.0 2.4 fusion.131
  131.0 3.2 %fusion.104 = f32[4,256,512]{2,1,0:T(8,128)} fusion(f32[512]{0:T(512)S(1)} %bitcast.192, f32[4,256]{1,0:T(4,128)S(1)} %add_rsqrt_fusion.7, bf16[4,3,512,512]{3,2,1,0:T(8,128)(2,1)} %all-gather.4.cloned.1.call-done, bf16[4,256,512]{2,1,0:T(8,128)(2,1)S(1)} %gather_fusion, pred[4]{0:T(512)(128)(4,1)S(1)} %get-tuple-element.210), kind=kOutput, calls=%fused_computation.135 | convolution fusion | flops 539492352 | bytes 3676164 | tf_op jit(solution)/shard_map/dot_general | solution.py:30
  134.2 3.1 %fusion.106 = f32[4,256,512]{2,1,0:T(8,128)} fusion(f32[512]{0:T(512)S(1)} %bitcast.193, f32[4,256]{1,0:T(4,128)S(1)} %add_rsqrt_fusion.7, bf16[4,3,512,512]{3,2,1,0:T(8,128)(2,1)} %all-gather.4.cloned.1.call-done, bf16[4,256,512]{2,1,0:T(8,128)(2,1)S(1)} %gather_fusion, pred[4]{0:T(512)(128)(4,1)S(1)} %get-tuple-element.210), kind=kOutput, calls=%fused_computation.136 | convolution fusion | flops 539492352 | bytes 3676164 | tf_op jit(solution)/shard_map/dot_general | solution.py:30
  137.3 4.6 %fusion.16 = (f32[4,256]{1,0:T(4,128)S(1)}, bf16[4,256,512]{2,1,0:T(8,128)(2,1)}) fusion(bf16[4,512,512]{2,1,0:T(8,128)(2,1)} %all-gather.6.cloned.1.call-done, f32[4,256,512]{2,1,0:T(8,128)} %fusion.104, f32[4,256,512]{2,1,0:T(8,128)} %fusion.106, f32[512]{0:T(512)S(1)} %bitcast.194, f32[4,256]{1,0:T(4,128)S(1)} %add_rsqrt_fusion.7, ...), kind=kOutput, calls=%fused_computation.54 | convolution fusion | flops 1083702272 | bytes 8399872 | tf_op jit(solution)/shard_map/dot_general | solution.py:36
  141.9 3.6 %fusion.82 = f32[4,256,512]{2,1,0:T(8,128)} fusion(bf16[4,256,512]{2,1,0:T(8,128)(2,1)} %get-tuple-element.196, f32[512]{0:T(512)S(1)} %bitcast.186, f32[4,256]{1,0:T(4,128)S(1)} %add_rsqrt_fusion.6, bf16[4,3,512,512]{3,2,1,0:T(8,128)(2,1)} %all-gather.4.cloned.1.call-done), kind=kOutput, calls=%fused_computation.119 | convolution fusion | flops 538968064 | bytes 3676160 | tf_op jit(solution)/shard_map/dot_general | solution.py:30
  145.5 3.1 %fusion.84 = f32[4,256,512]{2,1,0:T(8,128)} fusion(bf16[4,256,512]{2,1,0:T(8,128)(2,1)S(1)} %copy-done.15, f32[512]{0:T(512)S(1)} %bitcast.187, f32[4,256]{1,0:T(4,128)S(1)} %add_rsqrt_fusion.6, bf16[4,3,512,512]{3,2,1,0:T(8,128)(2,1)} %all-gather.4.cloned.1.call-done), kind=kOutput, calls=%fused_computation.120 | convolution fusion | flops 538968064 | bytes 3676160 | tf_op jit(solution)/shard_map/dot_general | solution.py:30
  148.7 4.3 %fusion.19 = bf16[4,256,512]{2,1,0:T(8,128)(2,1)S(1)} fusion(bf16[4,256,512]{2,1,0:T(8,128)(2,1)} %get-tuple-element.196, f32[4,256,512]{2,1,0:T(8,128)} %fusion.82, f32[4,256,512]{2,1,0:T(8,128)} %fusion.84, f32[512]{0:T(512)S(1)} %bitcast.188, f32[4,256]{1,0:T(4,128)S(1)} %add_rsqrt_fusion.6, bf16[4,3,512,512]{3,2,1,0:T(8,128)(2,1)} %all-gather.4.cloned.1.call-done, ...), kind=kOutput, calls=%fused_computation.57 | convolution fusion | flops 1081081856 | bytes 8394752 | tf_op jit(solution)/shard_map/dot_general | solution.py:36
  153.0 1.1 fusion.125
  155.3 0.7 broadcast_select_fusion.9
  156.3 6.6 %all-reduce.18 = (f32[8,18]{1,0:T(8,128)S(1)}, f32[8]{0:T(128)S(1)}) all-reduce(f32[8,18]{1,0:T(8,128)S(1)} %scatter-add.19, f32[8]{0:T(128)S(1)} %fusion.155), channel_id=1, replica_groups=mesh['section'=4,'dp_0'=4,'dp_1'=4,'dp_2'=2] {'section'}, use_global_device_ids=true, to_apply=%region_21.23 | all-reduce | flops 152 | bytes 1216 | tf_op jit(solution)/shard_map/psum | solution.py:19
  163.0 8.6 %all-reduce.17 = (f32[8,18]{1,0:T(8,128)S(1)}, f32[8]{0:T(128)S(1)}) all-reduce(f32[8,18]{1,0:T(8,128)S(1)} %get-tuple-element.167, f32[8]{0:T(128)S(1)} %get-tuple-element.168), channel_id=1, replica_groups=mesh['section'=4,'dp_0'=4,'dp_1'=4,'dp_2'=2] {'dp_0'}, use_global_device_ids=true, to_apply=%region_22.24 | all-reduce | flops 152 | bytes 1216 | tf_op jit(solution)/shard_map/psum | solution.py:19
  171.5 8.7 %all-reduce.16 = (f32[8,18]{1,0:T(8,128)S(1)}, f32[8]{0:T(128)S(1)}) all-reduce(f32[8,18]{1,0:T(8,128)S(1)} %get-tuple-element.165, f32[8]{0:T(128)S(1)} %get-tuple-element.166), channel_id=1, replica_groups=mesh['section'=4,'dp_0'=4,'dp_1'=4,'dp_2'=2] {'dp_1'}, use_global_device_ids=true, to_apply=%region_23.25 | all-reduce | flops 152 | bytes 1216 | tf_op jit(solution)/shard_map/psum | solution.py:19
  180.3 9.1 %all-reduce.19 = (f32[8,18]{1,0:T(8,128)S(1)}, f32[8]{0:T(128)S(1)}) all-reduce(f32[8,18]{1,0:T(8,128)S(1)} %get-tuple-element.163, f32[8]{0:T(128)S(1)} %get-tuple-element.164), channel_id=1, replica_groups=mesh['section'=4,'dp_0'=4,'dp_1'=4,'dp_2'=2] {'dp_2'}, use_global_device_ids=true, to_apply=%region_24.26 | all-reduce | flops 152 | bytes 1216 | tf_op jit(solution)/shard_map/psum | solution.py:19
  189.4 0.7 broadcast_select_fusion.11
  190.1 0.6 broadcast_select_fusion.8
  190.8 0.7 broadcast_select_fusion.7
  192.1 0.6 broadcast_select_fusion.5
  192.8 0.7 broadcast_select_fusion.4
  193.6 0.7 broadcast_select_fusion.3
  194.3 0.6 broadcast_select_fusion.2
  197.6 3.1 %fusion.120 = f32[4,256,512]{2,1,0:T(8,128)} fusion(bf16[4,256,512]{2,1,0:T(8,128)(2,1)S(1)} %bitcast.170, bf16[4,3,512,512]{3,2,1,0:T(8,128)(2,1)} %all-gather.4.cloned.1.call-done), kind=kOutput, calls=%fused_computation.160 | convolution fusion | flops 536870912 | bytes 3670016 | tf_op jit(solution)/shard_map/dot_general | solution.py:30
  200.7 3.1 %fusion.118 = f32[4,256,512]{2,1,0:T(8,128)} fusion(bf16[4,256,512]{2,1,0:T(8,128)(2,1)S(1)} %bitcast.171, bf16[4,3,512,512]{3,2,1,0:T(8,128)(2,1)} %all-gather.4.cloned.1.call-done), kind=kOutput, calls=%fused_computation.158 | convolution fusion | flops 536870912 | bytes 3670016 | tf_op jit(solution)/shard_map/dot_general | solution.py:30
  203.8 5.2 %fusion.28 = (f32[4,256]{1,0:T(4,128)S(1)}, bf16[4,256,512]{2,1,0:T(8,128)(2,1)}) fusion(f32[4,256,512]{2,1,0:T(8,128)} %bitcast.174, bf16[4,512,512]{2,1,0:T(8,128)(2,1)} %all-gather.6.cloned.1.call-done, f32[4,256,512]{2,1,0:T(8,128)} %fusion.120, f32[4,256,512]{2,1,0:T(8,128)} %fusion.118, bf16[4,256,512]{2,1,0:T(8,128)(2,1)S(1)} %bitcast.172, ...), kind=kOutput, calls=%fused_computation.66 | convolution fusion | flops 1080032256 | bytes 9441280 | tf_op jit(solution)/shard_map/dot_general | solution.py:36
  209.0 3.5 %fusion.48 = f32[4,256,512]{2,1,0:T(8,128)} fusion(bf16[4,256,512]{2,1,0:T(8,128)(2,1)} %get-tuple-element.202, f32[4,256]{1,0:T(4,128)S(1)} %add_rsqrt_fusion, f32[512]{0:T(512)S(1)} %bitcast.177, bf16[4,3,512,512]{3,2,1,0:T(8,128)(2,1)} %all-gather.4.cloned.1.call-done), kind=kOutput, calls=%fused_computation.103 | convolution fusion | flops 538968064 | bytes 3676160 | tf_op jit(solution)/shard_map/dot_general | solution.py:30
  212.5 3.2 %fusion.46 = f32[4,256,512]{2,1,0:T(8,128)} fusion(bf16[4,256,512]{2,1,0:T(8,128)(2,1)S(1)} %copy-done.14, f32[4,256]{1,0:T(4,128)S(1)} %add_rsqrt_fusion, f32[512]{0:T(512)S(1)} %bitcast.178, bf16[4,3,512,512]{3,2,1,0:T(8,128)(2,1)} %all-gather.4.cloned.1.call-done), kind=kOutput, calls=%fused_computation.102 | convolution fusion | flops 538968064 | bytes 3676160 | tf_op jit(solution)/shard_map/dot_general | solution.py:30
  215.7 3.8 %fusion.43 = f32[4,256]{1,0:T(4,128)S(1)} fusion(f32[4,256,512]{2,1,0:T(8,128)} %fusion.46, f32[4,256,512]{2,1,0:T(8,128)} %fusion.48, bf16[4,256,512]{2,1,0:T(8,128)(2,1)S(1)} %copy-done.14, f32[4,256]{1,0:T(4,128)S(1)} %add_rsqrt_fusion, f32[512]{0:T(512)S(1)} %bitcast.179, bf16[4,3,512,512]{3,2,1,0:T(8,128)(2,1)} %all-gather.4.cloned.1.call-done, ...), kind=kOutput, calls=%fused_computation.81 | convolution fusion | flops 1084226560 | bytes 8399360 | tf_op jit(solution)/shard_map/dot_general | solution.py:36
  219.5 3.0 %fusion.121 = f32[4,256,512]{2,1,0:T(8,128)} fusion(bf16[4,256,512]{2,1,0:T(8,128)(2,1)S(1)} %bitcast.167, bf16[4,3,512,512]{3,2,1,0:T(8,128)(2,1)} %all-gather.4.cloned.1.call-done), kind=kOutput, calls=%fused_computation.161 | convolution fusion | flops 536870912 | bytes 3670016 | tf_op jit(solution)/shard_map/dot_general | solution.py:30
  222.5 3.3 %fusion.119 = f32[4,256,512]{2,1,0:T(8,128)} fusion(bf16[4,256,512]{2,1,0:T(8,128)(2,1)S(1)} %bitcast.168, bf16[4,3,512,512]{3,2,1,0:T(8,128)(2,1)} %all-gather.4.cloned.1.call-done), kind=kOutput, calls=%fused_computation.159 | convolution fusion | flops 536870912 | bytes 3670016 | tf_op jit(solution)/shard_map/dot_general | solution.py:30
  225.8 4.4 %fusion.20 = (f32[4,256]{1,0:T(4,128)S(1)}, bf16[4,256,512]{2,1,0:T(8,128)(2,1)}) fusion(f32[4,256,512]{2,1,0:T(8,128)S(1)} %bitcast.173, bf16[4,512,512]{2,1,0:T(8,128)(2,1)} %all-gather.6.cloned.1.call-done, f32[4,256,512]{2,1,0:T(8,128)} %fusion.121, f32[4,256,512]{2,1,0:T(8,128)} %fusion.119, bf16[4,256,512]{2,1,0:T(8,128)(2,1)S(1)} %bitcast.169, ...), kind=kOutput, calls=%fused_computation.58 | convolution fusion | flops 1080032256 | bytes 9441280 | tf_op jit(solution)/shard_map/dot_general | solution.py:36
  230.2 3.6 %fusion.68 = f32[4,256,512]{2,1,0:T(8,128)} fusion(bf16[4,256,512]{2,1,0:T(8,128)(2,1)} %get-tuple-element.204, f32[512]{0:T(512)S(1)} %bitcast.180, f32[4,256]{1,0:T(4,128)S(1)} %add_rsqrt_fusion.4, bf16[4,3,512,512]{3,2,1,0:T(8,128)(2,1)} %all-gather.4.cloned.1.call-done), kind=kOutput, calls=%fused_computation.111 | convolution fusion | flops 538968064 | bytes 3676160 | tf_op jit(solution)/shard_map/dot_general | solution.py:30
  233.8 3.2 %fusion.70 = f32[4,256,512]{2,1,0:T(8,128)} fusion(bf16[4,256,512]{2,1,0:T(8,128)(2,1)S(1)} %copy-done.13, f32[512]{0:T(512)S(1)} %bitcast.181, f32[4,256]{1,0:T(4,128)S(1)} %add_rsqrt_fusion.4, bf16[4,3,512,512]{3,2,1,0:T(8,128)(2,1)} %all-gather.4.cloned.1.call-done), kind=kOutput, calls=%fused_computation.112 | convolution fusion | flops 538968064 | bytes 3676160 | tf_op jit(solution)/shard_map/dot_general | solution.py:30
  237.0 3.8 %fusion.37 = f32[4,256]{1,0:T(4,128)S(1)} fusion(f32[4,256,512]{2,1,0:T(8,128)} %fusion.68, f32[4,256,512]{2,1,0:T(8,128)} %fusion.70, bf16[4,256,512]{2,1,0:T(8,128)(2,1)S(1)} %copy-done.13, f32[512]{0:T(512)S(1)} %bitcast.182, f32[4,256]{1,0:T(4,128)S(1)} %add_rsqrt_fusion.4, bf16[4,3,512,512]{3,2,1,0:T(8,128)(2,1)} %all-gather.4.cloned.1.call-done, ...), kind=kOutput, calls=%fused_computation.75 | convolution fusion | flops 1084226560 | bytes 8399360 | tf_op jit(solution)/shard_map/dot_general | solution.py:36
  (78 shorter events, 6.8 us)
Async XLA Ops:
  7.2 187.9 %copy-start = (bf16[18,512]{1,0:T(8,128)(2,1)S(1)}, bf16[18,512]{1,0:T(8,128)(2,1)}, u32[]{:S(2)}) copy-start(bf16[18,512]{1,0:T(8,128)(2,1)} %param.43) | copy-start | bytes 55300
  7.2 1.5 copy-start.7
  7.2 12.6 %copy-start.8 = (s32[8,4]{0,1:T(4,128)S(1)}, s32[8,4]{0,1:T(4,128)}, u32[]{:S(2)}) copy-start(s32[8,4]{0,1:T(4,128)} %param.36) | copy-start | bytes 388
  7.2 71.3 %all-gather.4.cloned.1.call-start = ((), (), s32[]{:S(2)}) async-start(), calls=%async_computation | async-start | bytes 7864320 | tf_op jit(solution)/shard_map/all_gather | solution.py:100
  7.9 103.5 %all-gather.6.cloned.1.call-start = ((), (), s32[]{:S(2)}) async-start(), calls=%async_computation.1 | async-start | bytes 2621440 | tf_op jit(solution)/shard_map/all_gather | solution.py:101
  20.1 14.8 %copy-start.10 = (bf16[1,512]{1,0:T(2,128)(2,1)S(1)}, bf16[1,512]{1,0:T(2,128)(2,1)}, u32[]{:S(2)}) copy-start(bf16[1,512]{1,0:T(2,128)(2,1)} %param.40) | copy-start | bytes 3076
  20.1 25.6 %copy-start.9 = (s32[2]{0:T(128)S(1)}, s32[2]{0:T(128)}, u32[]{:S(2)}) copy-start(s32[2]{0:T(128)} %constant.322.clone.1) | copy-start | bytes 28
  24.8 112.5 %copy-start.5 = (bf16[4,256,512]{2,1,0:T(8,128)(2,1)}, bf16[4,256,512]{2,1,0:T(8,128)(2,1)S(1)}, u32[]{:S(2)}) copy-start(bf16[4,256,512]{2,1,0:T(8,128)(2,1)S(1)} %gather_fusion) | copy-start | bytes 3145732
  116.1 3.5 %copy-start.16 = (bf16[4,256,512]{2,1,0:T(8,128)(2,1)S(1)}, bf16[4,256,512]{2,1,0:T(8,128)(2,1)}, u32[]{:S(2)}) copy-start(bf16[4,256,512]{2,1,0:T(8,128)(2,1)} %get-tuple-element.194) | copy-start | bytes 3145732
  122.8 5.2 %copy-start.11 = (bf16[512,18]{0,1:T(8,128)(2,1)S(1)}, bf16[512,18]{0,1:T(8,128)(2,1)}, u32[]{:S(2)}) copy-start(bf16[512,18]{0,1:T(8,128)(2,1)} %param.41) | copy-start | bytes 55300
  122.8 5.2 %copy-start.12 = (f32[18]{0:T(128)S(1)}, f32[18]{0:T(128)}, u32[]{:S(2)}) copy-start(f32[18]{0:T(128)} %param.42) | copy-start | bytes 220
  141.9 3.6 %copy-start.15 = (bf16[4,256,512]{2,1,0:T(8,128)(2,1)S(1)}, bf16[4,256,512]{2,1,0:T(8,128)(2,1)}, u32[]{:S(2)}) copy-start(bf16[4,256,512]{2,1,0:T(8,128)(2,1)} %get-tuple-element.196) | copy-start | bytes 3145732
  195.7 1.4 copy-start.2
  196.2 1.4 copy-start.4
  209.0 3.5 %copy-start.14 = (bf16[4,256,512]{2,1,0:T(8,128)(2,1)S(1)}, bf16[4,256,512]{2,1,0:T(8,128)(2,1)}, u32[]{:S(2)}) copy-start(bf16[4,256,512]{2,1,0:T(8,128)(2,1)} %get-tuple-element.202) | copy-start | bytes 3145732
  222.5 3.3 %copy-start.3 = (f32[1024,512]{1,0:T(8,128)S(1)}, f32[1024,512]{1,0:T(8,128)}, u32[]{:S(2)}) copy-start(f32[1024,512]{1,0:T(8,128)} %copy-done.2) | copy-start | bytes 6291460
  230.2 3.6 %copy-start.13 = (bf16[4,256,512]{2,1,0:T(8,128)(2,1)S(1)}, bf16[4,256,512]{2,1,0:T(8,128)(2,1)}, u32[]{:S(2)}) copy-start(bf16[4,256,512]{2,1,0:T(8,128)(2,1)} %get-tuple-element.204) | copy-start | bytes 3145732
  233.8 3.2 %copy-start.6 = (bf16[4,256,512]{2,1,0:T(8,128)(2,1)S(1)}, bf16[4,256,512]{2,1,0:T(8,128)(2,1)}, u32[]{:S(2)}) copy-start(bf16[4,256,512]{2,1,0:T(8,128)(2,1)} %copy-done.5) | copy-start | bytes 3145732
  237.0 4.9 %copy-start.1 = (bf16[18,512]{1,0:T(8,128)(2,1)S(1)}, bf16[18,512]{1,0:T(8,128)(2,1)}, u32[]{:S(2)}) copy-start(bf16[18,512]{1,0:T(8,128)(2,1)} %param.43) | copy-start | bytes 55300
Sparse Core Ops, SparseCore 0:
  9.7 68.7 all-gather.3
  80.1 31.2 all-gather.5
where the time goes:
time: 250 us; the launch traced here: 249 us
  matrix products  92.5 us (37%)
  waiting for transfers between devices  58.3 us (23%)
  blocking collectives  43.8 us (18%)
  between operations  31.2 us (12%)
  local copies, waits for them, and re-layouts  11.8 us (5%)
  other arithmetic  11.1 us (4%)
    dot_general x16, matrix products, run_block(): jnp.dot(flat, tap_set[k], preferred_element_type=jnp.float32)  52 us
    dot_general x8, matrix products, run_block(): jnp.dot(activated.reshape(-1, channels), out_weight, preferred_element_ty...  35.9 us
    psum x4, blocking collectives, over_axes(): return functools.reduce(lax.psum, axes, array)  33 us
    all_gather x1, waiting for transfers between devices, on_device(): lax.all_gather(tap_weights, 'section', axis=0, tiled=True)  30.2 us
    all_gather x1, waiting for transfers between devices, on_device(): lax.all_gather(out_weights, 'section', axis=0, tiled=True)  26.6 us
    all_gather x1, blocking collectives, on_device(): lax.all_gather(norm_gains, 'section', axis=0, tiled=True)  10.8 us
    gather x2, local copies, waits for them, and re-layouts, on_device(): source = jnp.take(clip_pool, clip_index[batch_slot], axis=0)  9.48 us
    another operation x12, other arithmetic  8.18 us
  transfers between devices with their start and end apart: 2, of which 2 were waited for; matrix products, arithmetic and copies ran while one was open for 8% of the time, Pallas kernels for 0%

commit v1 on v0

v1 whole, which is shorter than its diff:
```python
import functools

import jax
import jax.numpy as jnp
from jax import lax
from jax.experimental import pallas as pl
from jax.experimental.pallas import tpu as pltpu
from jax.sharding import Mesh
from jax.sharding import PartitionSpec as P


DP = ("dp_0", "dp_1", "dp_2")
MESH = pl.DeviceIdType.MESH
F32 = jnp.float32
BF16 = jnp.bfloat16
C = 512
BITS = 18
CLIPS = 4
ROWS = 256
SPATIAL = 64
GROUP = CLIPS * ROWS
NORM_EPS = 1e-06
ROWS_TOTAL = 128.0 * 256.0


def dot(a, b):
    return jnp.dot(a, b, preferred_element_type=F32)


def silu(u):
    return 0.5 * u * (1.0 + jnp.tanh(0.5 * u))


def rows_of(value, first, count):
    parts = value.reshape(CLIPS, -1, value.shape[-1])
    return parts[:, first : first + count].reshape(CLIPS * count, value.shape[-1])


def normalize(v, gain):
    wide = v.astype(F32)
    mean = jnp.mean(wide * wide, axis=-1, keepdims=True)
    return (wide * lax.rsqrt(mean + NORM_EPS) * gain).astype(BF16)


def taps(n, weight):
    p0 = dot(n, weight(0)).reshape(CLIPS, ROWS, C)
    p1 = dot(rows_of(n, 0, ROWS - SPATIAL), weight(1)).reshape(CLIPS, ROWS - SPATIAL, C)
    p2 = dot(rows_of(n, 0, ROWS - 2 * SPATIAL), weight(2)).reshape(CLIPS, ROWS - 2 * SPATIAL, C)
    mixed = jnp.concatenate(
        [
            p0[:, :SPATIAL],
            p0[:, SPATIAL : 2 * SPATIAL] + p1[:, :SPATIAL],
            p0[:, 2 * SPATIAL :] + p1[:, SPATIAL:] + p2,
        ],
        axis=1,
    )
    return mixed.reshape(GROUP, C)


def kernel(
    index_ref, order_ref, pool_hbm, taps_hbm, out_hbm, gains_hbm, qw_hbm, qb_hbm, pw_hbm,
    error_ref, loss_ref,
    pool, wts, gains, act, acc, qw, qb, pw, qwp, pwp, stat1, stat2,
    lsem, xs, xr, gs, gr, rs, rr, ds, dr, s1s, s1r, s2s, s2r,
):
    x = lax.axis_index("section")
    y = lax.axis_index("dp_0")
    z = lax.axis_index("dp_1")
    c = lax.axis_index("dp_2")
    q = y * (1 - c) + z * c

    def xpeer(d):
        return (lax.rem(x + d, 4), y, z, c)

    def ring(d):
        return (x, lax.rem(y + d * (1 - c), 4), lax.rem(z + d * c, 4), c)

    def plane(dy, dz):
        return (x, lax.rem(y + dy, 4), lax.rem(z + dz, 4), c)

    def other(d, e):
        return (lax.rem(x + d, 4), y, z, lax.rem(c + e, 2))

    sibling = other(0, 1)
    planes = [(dy, dz) for dy in range(4) for dz in range(4) if dy or dz]
    others = [(d, e) for d in range(4) for e in range(2) if d or e]

    loads = [
        (taps_hbm.at[0], wts.at[x, pl.ds(0, 3)]),
        (out_hbm.at[0], wts.at[x, 3]),
        (gains_hbm, gains.at[x]),
        (pool_hbm, pool),
        (qw_hbm, qw),
        (qb_hbm, qb),
        (pw_hbm, pw),
    ]
    loads = [pltpu.make_async_copy(a, b, lsem.at[i]) for i, (a, b) in enumerate(loads)]
    for load in loads:
        load.start()
    barrier = pltpu.get_barrier_semaphore()
    for dy, dz in planes:
        pl.semaphore_signal(barrier, inc=1, device_id=plane(dy, dz), device_id_type=MESH)
    for d, e in others:
        pl.semaphore_signal(barrier, inc=1, device_id=other(d, e), device_id_type=MESH)
    pl.semaphore_wait(barrier, len(planes) + len(others))
    for load in loads[:3]:
        load.wait()

    def remote(ref, send, recv, device):
        return pltpu.make_async_remote_copy(
            ref, ref, send, recv, device_id=device, device_id_type=MESH
        )

    def quarter(b, m, owner):
        return wts.at[b, m, pl.ds(pl.multiple_of(c * 256 + owner * 64, 64), 64)]

    def xcopy(b, m, d):
        return remote(quarter(b, m, q), xs.at[m, d - 1], xr.at[b, m], xpeer(d))

    def gcopy(b, d):
        return remote(gains.at[b], gs.at[d - 1], gr.at[b], xpeer(d))

    def rcopy(b, m, d, owner):
        return remote(quarter(b, m, owner), rs.at[b, m, d - 1], rr.at[b, m, d - 1], ring(d))

    def dcopy(b, m, h):
        ref = wts.at[b, m, pl.ds(pl.multiple_of(h * 256, 256), 256)]
        return remote(ref, ds.at[b, m], dr.at[b, m], sibling)

    def own(m, *distances):
        for d in distances:
            xcopy(x, m, d).start()

    for d in (1, 3, 2):
        gcopy(x, d).start()

    @pl.when(x == 0)
    def _():
        for m in range(4):
            own(m, 1, 3, 2)

    @pl.when(x == 1)
    def _():
        for m in range(4):
            own(m, 3)

    def X(b, m):
        @pl.when(x != b)
        def _():
            xcopy(b, m, 1).wait_recv()
            for d in (1, 3, 2):
                rcopy(b, m, d, q).start()

        if b == 0:

            @pl.when(x == 1)
            def _():
                own(m, 1, 2)

            @pl.when(x == 2)
            def _():
                own(m, 3, 1, 2)

        if b == 1:

            @pl.when(x == 3)
            def _():
                own(m, 1, 3, 2)

    def R(b, m):
        @pl.when(x != b)
        def _():
            for d in (1, 3, 2):
                rcopy(b, m, d, lax.rem(q + 4 - d, 4)).wait_recv()
            dcopy(b, m, c).start()

    def D(b, m):
        @pl.when(x != b)
        def _():
            dcopy(b, m, 1 - c).wait_recv()
            if m == 0:
                gcopy(b, 1).wait_recv()

    def group(g):
        return pl.ds(g * GROUP, GROUP)

    def gain(b):
        return gains[b].astype(F32)

    def source(i, k):
        return pool[index_ref[2 * x + i, k]]

    def weight(b):
        return lambda m: wts[b, m]

    def c0(m, g):
        def part(n, skip):
            product = dot(rows_of(n, 0, ROWS - skip), wts[0, m]).reshape(CLIPS, ROWS - skip, C)
            for k in range(CLIPS):
                at = pl.ds(g * GROUP + k * ROWS + skip, ROWS - skip)
                acc[at, :] = acc[at, :] + product[k]

        if m == 0:
            for k in range(CLIPS):
                at = pl.ds(g * GROUP + k * ROWS, ROWS)
                act[at, :] = normalize(source(g, k), gain(0))
            acc[group(g), :] = dot(act[group(g), :], wts[0, 0])
        elif m < 3:
            part(act[group(g), :], m * SPATIAL)
        else:
            v = jnp.concatenate([source(g, k) for k in range(CLIPS)], axis=0)
            a = silu(acc[group(g), :]).astype(BF16)
            act[group(g), :] = (v.astype(F32) + dot(a, wts[0, 3])).astype(BF16)

    def cb(b, g):
        v = act[group(g), :]
        n = normalize(v, gain(b))
        a = silu(taps(n, weight(b))).astype(BF16)
        act[group(g), :] = (v.astype(F32) + dot(a, wts[b, 3])).astype(BF16)

    lane = lax.broadcasted_iota(jnp.int32, (8, 128), 1)
    row = lax.broadcasted_iota(jnp.int32, (8, 128), 0)

    def quantize(g):
        t = 4.0 * (dot(act[group(g), :], qwp[...]) + qb[...])
        codes = jnp.tanh(0.5 * t)
        act[group(g), :] = dot(codes.astype(BF16), pwp[...]).astype(BF16)
        size = jnp.abs(t)
        e = jnp.exp(-size)
        entropy = jnp.log(1.0 + e) + size * e / (1.0 + e)
        bit = jnp.sum(0.5 * (1.0 + codes), axis=0, keepdims=True)
        ent = jnp.sum(entropy, axis=0, keepdims=True)
        ent = jnp.sum(jnp.where(lane[:1] < BITS, ent, 0.0), axis=1, keepdims=True)
        both = jnp.where(lane[:1] < BITS, bit, jnp.where(lane[:1] == BITS, ent, 0.0))
        return jnp.where(row == 2 * x + g, both, 0.0)

    def s1copy(dy, dz, sy, sz):
        k = dy * 4 + dz
        ref = stat1.at[sy * 4 + sz]
        return remote(ref, s1s.at[k], s1r.at[k], plane(dy, dz))

    def s2copy(d, e, sx, sc):
        k = d * 2 + e
        ref = stat2.at[sx * 2 + sc]
        return remote(ref, s2s.at[k], s2r.at[k], other(d, e))

    def errors(g):
        for k in range(CLIPS):
            at = pl.ds(g * GROUP + k * ROWS, ROWS)
            differ = act[at, :].astype(F32) - source(g, k).astype(F32)
            square = differ * differ
            part = square[:, :128] + square[:, 128:256] + square[:, 256:384] + square[:, 384:]
            total = jnp.sum(part.T, axis=0, keepdims=True)
            error_ref[g, k : k + 1, :] = total * (1.0 / C)

    X(0, 0)
    X(0, 1)
    R(0, 0)
    X(0, 2)
    D(0, 0)
    loads[3].wait()
    c0(0, 0)
    R(0, 1)
    X(0, 3)
    c0(0, 1)
    X(1, 0)
    D(0, 1)
    c0(1, 0)
    R(0, 2)
    c0(1, 1)
    X(1, 1)
    D(0, 2)
    c0(2, 0)
    R(0, 3)
    c0(2, 1)
    X(1, 2)
    D(0, 3)
    c0(3, 0)
    R(1, 0)
    X(1, 3)
    c0(3, 1)
    for load in loads[4:]:
        load.wait()
    qwp[...] = jnp.zeros_like(qwp)
    pwp[...] = jnp.zeros_like(pwp)
    qwp[:, 0:BITS] = qw[...]
    pwp[0:BITS, :] = pw[...]
    R(1, 1)
    X(2, 0)
    D(1, 0)
    R(1, 2)
    D(1, 1)
    X(2, 1)
    R(1, 3)
    D(1, 2)
    X(2, 2)
    D(1, 3)
    cb(1, 0)
    R(2, 0)
    R(2, 1)
    X(2, 3)
    cb(1, 1)
    R(2, 2)
    D(2, 0)
    stats = quantize(0) + quantize(1)
    stat1[y * 4 + z] = stats
    R(2, 3)
    D(2, 1)
    X(3, 0)
    X(3, 1)
    D(2, 2)
    D(2, 3)
    cb(2, 0)
    for dy, dz in planes:
        s1copy(dy, dz, y, z).start()
    X(3, 2)
    R(3, 0)
    X(3, 3)
    R(3, 1)
    cb(2, 1)
    for dy, dz in planes:
        s1copy(dy, dz, lax.rem(y + 4 - dy, 4), lax.rem(z + 4 - dz, 4)).wait_recv()
    total = stat1[0]
    for k in range(1, 16):
        total = total + stat1[k]
    stat2[x * 2 + c] = total
    R(3, 2)
    D(3, 0)
    R(3, 3)
    D(3, 1)
    D(3, 2)
    D(3, 3)
    for d, e in others:
        s2copy(d, e, x, c).start()
    cb(3, 0)
    errors(0)
    cb(3, 1)
    errors(1)

    for d, e in others:
        s2copy(d, e, lax.rem(x + 4 - d, 4), lax.rem(c + 2 - e, 2)).wait_recv()
    total = stat2[0]
    for k in range(1, 8):
        total = total + stat2[k]
    mean = total / ROWS_TOTAL
    averaged = jnp.zeros((8, 128), F32)
    running = None
    for t in range(8):
        chosen = row == order_ref[t]
        marginal = jnp.sum(jnp.where(chosen, mean, 0.0), axis=0, keepdims=True)
        running = marginal if t == 0 else 0.5 * running + 0.5 * marginal
        averaged = jnp.where(chosen, running, averaged)
    smoothed = 0.05 + 0.9 * averaged
    smoothed = jnp.where(lane < BITS, smoothed, 0.5)
    terms = smoothed * jnp.log(smoothed) + (1.0 - smoothed) * jnp.log(1.0 - smoothed)
    terms = jnp.where(lane < BITS, terms, jnp.where(lane == BITS, mean, 0.0))
    loss_ref[...] = jnp.sum(terms, axis=1, keepdims=True) + jnp.zeros((8, 128), F32)

    for d in (1, 3, 2):
        gcopy(x, d).wait_send()
        for m in range(4):
            xcopy(x, m, d).wait_send()
    for b in range(4):

        @pl.when(x != b)
        def _():
            for m in range(4):
                for d in (1, 3, 2):
                    rcopy(b, m, d, q).wait_send()
                dcopy(b, m, c).wait_send()

    for dy, dz in planes:
        s1copy(dy, dz, y, z).wait_send()
    for d, e in others:
        s2copy(d, e, x, c).wait_send()


def on_device(
    clip_pool, clip_index, batch_order, tap_weights, out_weights, norm_gains,
    quant_weight, quant_bias, post_weight,
):
    any_space = pl.BlockSpec(memory_space=pl.ANY)
    smem = pl.BlockSpec(memory_space=pltpu.SMEM)
    vmem = pl.BlockSpec(memory_space=pltpu.VMEM)
    dma = pltpu.SemaphoreType.DMA
    bias = jnp.zeros((1, 128), F32).at[0, :BITS].set(quant_bias)
    error, loss = pl.pallas_call(
        kernel,
        out_shape=(
            jax.ShapeDtypeStruct((2, CLIPS, ROWS), F32),
            jax.ShapeDtypeStruct((8, 128), F32),
        ),
        in_specs=[smem, smem] + [any_space] * 7,
        out_specs=(vmem, vmem),
        scratch_shapes=[
            pltpu.VMEM((32, ROWS, C), BF16),
            pltpu.VMEM((4, 4, C, C), BF16),
            pltpu.VMEM((4, 1, C), BF16),
            pltpu.VMEM((2 * GROUP, C), BF16),
            pltpu.VMEM((2 * GROUP, C), F32),
            pltpu.VMEM((C, BITS), BF16),
            pltpu.VMEM((1, 128), F32),
            pltpu.VMEM((BITS, C), BF16),
            pltpu.VMEM((C, 128), BF16),
            pltpu.VMEM((128, C), BF16),
            pltpu.VMEM((16, 8, 128), F32),
            pltpu.VMEM((8, 8, 128), F32),
            dma((7,)),
            dma((4, 3)),
            dma((4, 4)),
            dma((3,)),
            dma((4,)),
            dma((4, 4, 3)),
            dma((4, 4, 3)),
            dma((4, 4)),
            dma((4, 4)),
            dma((16,)),
            dma((16,)),
            dma((8,)),
            dma((8,)),
        ],
        compiler_params=pltpu.CompilerParams(
            collective_id=0, has_side_effects=True, vmem_limit_bytes=60 * 2**20
        ),
    )(
        clip_index, batch_order, clip_pool, tap_weights, out_weights, norm_gains,
        quant_weight, bias, post_weight,
    )
    return error, loss[:, 0]


def solution(mesh):
    torus = Mesh(
        mesh.devices.reshape(mesh.shape["section"], 4, 4, 2), ("section", "dp_0", "dp_1", "dp_2")
    )
    return jax.shard_map(
        on_device,
        mesh=torus,
        in_specs=(
            P(DP, None, None),
            P(None, DP),
            P(),
            P("section", None, None, None),
            P("section", None, None),
            P("section", None),
            P(),
            P(),
            P(),
        ),
        out_specs=(P("section", DP, None), P()),
        check_vma=False,
    )
```

time: 250 us -> 66.3 us (0.27)
  matrix products: 92.5 us -> 0 us
  waiting for transfers between devices: 58.3 us -> 0 us
  Pallas kernels: 0 us -> 57.4 us
  blocking collectives: 43.8 us -> 0 us
  between operations: 31.2 us -> 0.64 us
  other arithmetic: 11.1 us -> 1.95 us
  local copies, waits for them, and re-layouts: 11.8 us -> 5.97 us
    dot_general x28 -> x0, matrix products: 92.5 us -> none  [the longest x16 52 us: run_block(): jnp.dot(flat, tap_set[k], preferred_element_type=jnp.float32)]
    pallas_call x0 -> x1, Pallas kernels: none -> 57.4 us  [on_device(): pl.pallas_call(kernel, out_shape=(jax.ShapeDtypeStruct((2, CLIPS, ROWS),...]
    all_gather x2 -> x0, waiting for transfers between devices: 56.9 us -> none  [the longest x1 30.2 us: on_device(): lax.all_gather(tap_weights, 'section', axis=0, tiled=True)]
    psum x4 -> x0, blocking collectives: 33 us -> none  [over_axes(): return functools.reduce(lax.psum, axes, array)]
    all_gather x1 -> x0, blocking collectives: 10.8 us -> none  [on_device(): lax.all_gather(norm_gains, 'section', axis=0, tiled=True)]
    gather x2 -> x0, local copies, waits for them, and re-layouts: 9.48 us -> none  [on_device(): source = jnp.take(clip_pool, clip_index[batch_slot], axis=0)]
    another operation x13 -> x2, other arithmetic: 8.78 us -> 1.95 us
    unnamed x34 -> x3, local copies, waits for them, and re-layouts: 1.01 us -> 4.14 us
  transfers between devices with their start and end apart: 2 -> 0, of which waited for: 2 -> 0; matrix products, arithmetic and copies ran while one was open for 8% -> 0% of each run, Pallas kernels for 0% -> 0%
where the time goes in v1:
time: 66.3 us; the launch traced here: 66 us
  Pallas kernels  57.4 us (87%)
  local copies, waits for them, and re-layouts  5.97 us (9%)
  other arithmetic  1.95 us (3%)
    pallas_call x1, Pallas kernels, on_device(): pl.pallas_call(kernel, out_shape=(jax.ShapeDtypeStruct((2, CLIPS, ROWS),...  57.4 us
    unnamed x3, local copies, waits for them, and re-layouts  4.14 us
    another operation x2, other arithmetic  1.95 us

profile of v1, /device:TPU:1, one launch (start us, length us, event | category | flops | bytes accessed | tf_op | source)
XLA Modules:
  0.0 66.0 jit_solution(12198598232592451674)
XLA Ops:
  0.6 0.6 compare_reduce_fusion
  1.3 1.3 %fusion = f32[1,18]{1,0:T(1,128)S(1)} fusion(f32[18]{0:T(128)} %param.18, pred[]{:T(512)} %compare_reduce_fusion), kind=kLoop, calls=%fused_computation.3 | loop fusion | flops 18 | bytes 145 | tf_op jit(solution)/shard_map/reshape.29
  2.6 0.5 scatter.4.qb_hbm
  3.1 1.3 %copy.13.index_ref = s32[8,4]{1,0:T(8,128)} copy(s32[8,4]{0,1:T(4,128)} %param.12) | data formatting | bytes 256 | tf_op args[1]
  4.4 1.5 %copy.14.qw_hbm = bf16[512,18]{1,0:T(8,128)(2,1)} copy(bf16[512,18]{0,1:T(8,128)(2,1)} %param.17) | data formatting | bytes 36864 | tf_op args[6]
  5.9 57.4 %shard_map.104 = (f32[2,4,256]{2,1,0:T(4,128)}, f32[8,128]{1,0:T(8,128)}) custom-call(s32[8,4]{1,0:T(8,128)} %copy.13.index_ref, s32[8]{0:T(128)} %order_ref.1, bf16[32,256,512]{2,1,0:T(8,128)(2,1)} %pool_hbm.1, bf16[1,3,512,512]{3,2,1,0:T(8,128)(2,1)} %taps_hbm.1, bf16[1,512,512]{2,1,0:T(8,128)(2,1)} %out_hbm.1, bf16[1,512]{1,0:T(2,128)(2,1)} %gains_hbm.1, ...), custom_call_target="tpu_custom_call" | custom-call | tf_op jit(solution)/shard_map/pallas_call | solution.py:387
  63.4 1.3 %slice_reduce_fusion = f32[8]{0:T(128)} fusion(f32[8,128]{1,0:T(8,128)} %get-tuple-element.17), kind=kLoop, calls=%fused_computation | loop fusion | bytes 64 | tf_op jit(solution)/shard_map/slice | solution.py:429
  64.7 1.3 %copy.16 = f32[2,4,256]{2,1,0:T(4,128)} copy(f32[2,4,256]{2,1,0:T(4,128)} %get-tuple-element.20) | data formatting | bytes 16384

commit v2 on v1

v2 whole, which is shorter than its diff:
```python
import functools

import jax
import jax.numpy as jnp
from jax import lax
from jax.experimental import pallas as pl
from jax.experimental.pallas import tpu as pltpu
from jax.sharding import Mesh
from jax.sharding import PartitionSpec as P


DP = ("dp_0", "dp_1", "dp_2")
MESH = pl.DeviceIdType.MESH
F32 = jnp.float32
BF16 = jnp.bfloat16
C = 512
BITS = 18
PAD = 32
CLIPS = 4
ROWS = 256
SPATIAL = 64
GROUP = CLIPS * ROWS
NORM_EPS = 1e-06
ROWS_TOTAL = 128.0 * 256.0
DIRECT = (0, 2)

SCHEDULE = (
    ("V", 0), ("X", 0, 0), ("Y", 0), ("V", 1), ("V", 2), ("X", 0, 1), ("Y", 1), ("V", 3), ("X", 0, 2),
    ("Y", 2), ("X", 0, 3), ("Y", 3), ("R", 0, 0), ("X", 1, 0), ("X", 1, 1), ("Z", 0), ("Z", 1), ("R", 0, 1),
    ("E", 0, 0), ("pool",), ("cs", 0, 0, 0), ("cs", 0, 0, 1), ("R", 0, 2), ("X", 1, 2), ("Z", 2), ("Z", 3),
    ("E", 0, 1), ("cs", 0, 1, 0), ("cs", 0, 1, 1), ("R", 0, 3), ("X", 1, 3), ("E", 0, 2), ("cs", 0, 2, 0),
    ("X", 2, 0), ("cs", 0, 2, 1), ("R", 1, 0), ("E", 0, 3), ("cs", 0, 3, 0), ("X", 2, 1), ("cs", 0, 3, 1),
    ("prep",), ("R", 1, 1), ("X", 2, 2), ("L", 0), ("E", 1, 0), ("cs", 1, 0, 0), ("R", 1, 2), ("X", 2, 3),
    ("cs", 1, 0, 1), ("E", 1, 1), ("cs", 1, 1, 0), ("R", 1, 3), ("cs", 1, 1, 1), ("E", 1, 2), ("cs", 1, 2, 0),
    ("R", 2, 0), ("cs", 1, 2, 1), ("E", 1, 3), ("cs", 1, 3, 0), ("R", 2, 1), ("cs", 1, 3, 1), ("R", 2, 2),
    ("quant",), ("s1send",), ("R", 2, 3), ("L", 1), ("E", 2, 0), ("E", 2, 1), ("E", 2, 2), ("E", 2, 3),
    ("cb", 2, 0), ("cb", 2, 1), ("s1take",), ("s2send",), ("L", 2), ("cb", 3, 0), ("err", 0), ("cb", 3, 1),
    ("err", 1),
)


def dot(a, b):
    return jnp.dot(a, b, preferred_element_type=F32)


def dot_t(a, b):
    return lax.dot_general(a, b, (((1,), (1,)), ((), ())), preferred_element_type=F32)


def silu(u):
    return 0.5 * u * (1.0 + jnp.tanh(0.5 * u))


def rows_of(value, first, count):
    parts = value.reshape(CLIPS, -1, value.shape[-1])
    return parts[:, first : first + count].reshape(CLIPS * count, value.shape[-1])


def normalize(v, gain):
    wide = v.astype(F32)
    mean = jnp.mean(wide * wide, axis=-1, keepdims=True)
    return (wide * lax.rsqrt(mean + NORM_EPS) * gain).astype(BF16)


def taps(n, weight):
    p0 = dot(n, weight(0)).reshape(CLIPS, ROWS, C)
    p1 = dot(rows_of(n, 0, ROWS - SPATIAL), weight(1)).reshape(CLIPS, ROWS - SPATIAL, C)
    p2 = dot(rows_of(n, 0, ROWS - 2 * SPATIAL), weight(2)).reshape(CLIPS, ROWS - 2 * SPATIAL, C)
    mixed = jnp.concatenate(
        [
            p0[:, :SPATIAL],
            p0[:, SPATIAL : 2 * SPATIAL] + p1[:, :SPATIAL],
            p0[:, 2 * SPATIAL :] + p1[:, SPATIAL:] + p2,
        ],
        axis=1,
    )
    return mixed.reshape(GROUP, C)


def kernel(
    index_hbm, order_hbm, pool_hbm, taps_hbm, out_hbm, gains_hbm, qw_hbm, qb_hbm, pw_hbm,
    error_hbm, loss_hbm,
    pool, wts, gains, act, nrm, acc, index_ref, order_ref, qb, qw, pw, qwp, pwp, stat1, stat2, error_ref, loss_ref,
    lsem, osem, xs, xr, ys, zs, gs, gr, rs, rr, ds, dr, s1s, s1r, s2s, s2r,
):
    x = lax.axis_index("section")
    y = lax.axis_index("dp_0")
    z = lax.axis_index("dp_1")
    c = lax.axis_index("dp_2")
    q = y * (1 - c) + z * c

    def xpeer(d):
        return (lax.rem(x + d, 4), y, z, c)

    def ring(d):
        return (x, lax.rem(y + d * (1 - c), 4), lax.rem(z + d * c, 4), c)

    def plane(dy, dz):
        return (x, lax.rem(y + dy, 4), lax.rem(z + dz, 4), c)

    def other(d, e):
        return (lax.rem(x + d, 4), y, z, lax.rem(c + e, 2))

    sibling = other(0, 1)
    near = [(d, 0) for d in (1, 2, 3)] + [(0, d) for d in (1, 2, 3)]
    planes = [(dy, dz) for dy in range(4) for dz in range(4) if dy or dz]
    others = [(d, e) for d in range(4) for e in range(2) if d or e]

    barrier = pltpu.get_barrier_semaphore()
    for dy, dz in near:
        pl.semaphore_signal(barrier, inc=1, device_id=plane(dy, dz), device_id_type=MESH)
    for d, e in others:
        pl.semaphore_signal(barrier, inc=1, device_id=other(d, e), device_id_type=MESH)
    loads = [
        (taps_hbm.at[0], wts.at[x, pl.ds(0, 3)]),
        (out_hbm.at[0], wts.at[x, 3]),
        (gains_hbm, gains.at[x]),
        (index_hbm, index_ref),
        (pool_hbm, pool),
        (order_hbm, order_ref),
        (qb_hbm, qb),
        (qw_hbm, qw),
        (pw_hbm, pw),
    ]
    loads = [pltpu.make_async_copy(a, b, lsem.at[i]) for i, (a, b) in enumerate(loads)]
    for load in loads:
        load.start()
    with jax.named_scope("barrier"):
        pl.semaphore_wait(barrier, len(near) + len(others))
    for load in loads[:3]:
        load.wait()

    def remote(ref, send, recv, device):
        return pltpu.make_async_remote_copy(
            ref, ref, send, recv, device_id=device, device_id_type=MESH
        )

    def quarter(b, m, owner):
        return wts.at[b, m, pl.ds(pl.multiple_of(c * 256 + owner * 64, 64), 64)]

    def xcopy(b, m, d):
        return remote(quarter(b, m, q), xs.at[m, d // 2], xr.at[b, m], xpeer(d))

    def relay(m):
        b = 3 - x
        return remote(quarter(b, m, q), ys.at[m], xr.at[b, m], xpeer(1 + 2 * lax.rem(x, 2)))

    def across(m):
        return remote(quarter(0, m, q), zs.at[m], xr.at[0, m], xpeer(2))

    def gcopy(b, d):
        return remote(gains.at[b], gs.at[d - 1], gr.at[b], xpeer(d))

    def rcopy(b, m, d, owner):
        return remote(quarter(b, m, owner), rs.at[b, m, d - 1], rr.at[b, m, d - 1], ring(d))

    def dcopy(b, m, h):
        ref = wts.at[b, m, pl.ds(pl.multiple_of(h * 256, 256), 256)]
        return remote(ref, ds.at[b, m], dr.at[b, m], sibling)

    def foreign(f):
        return jnp.where(x <= f, f + 1, f)

    def own(m, d):
        xcopy(x, m, d).start()

    for m in range(4):

        @pl.when(x == 0)
        def _():
            own(m, 1)
            own(m, 3)
            if m in DIRECT:
                across(m).start()

        @pl.when(x == 1)
        def _():
            own(m, 3)
            own(m, 1)

        @pl.when(x == 2)
        def _():
            own(m, 3)

        @pl.when(x == 3)
        def _():
            own(m, 1)

    for d in (1, 3, 2):
        gcopy(x, d).start()

    def take(f, m):
        xcopy(foreign(f), m, 1).wait_recv()

    def V(m):
        @pl.when(x == 2)
        def _():
            take(1, m)
            relay(m).start()
            if m == 3:
                for k in range(4):
                    own(k, 1)

    def Y(m):
        @pl.when(x == 1)
        def _():
            take(1, m)
            relay(m).start()

    def Z(m):
        @pl.when(x == 0)
        def _():
            take(2, m)
            relay(m).start()

    def X(f, m):
        if f == 0:
            take(f, m)

            @pl.when(x == 3)
            def _():
                if m not in DIRECT:
                    relay(m).start()
                if m == 3:
                    for k in range(4):
                        own(k, 3)

        elif f == 1:

            @pl.when((x == 0) | (x == 3))
            def _():
                take(f, m)
        else:

            @pl.when(x > 0)
            def _():
                take(f, m)

        for d in (1, 3, 2):
            rcopy(foreign(f), m, d, q).start()

    def R(f, m):
        for d in (1, 3, 2):
            rcopy(foreign(f), m, d, lax.rem(q + 4 - d, 4)).wait_recv()
        dcopy(foreign(f), m, c).start()

    def landed(f, m):
        dcopy(foreign(f), m, 1 - c).wait_recv()
        if m == 0:
            gcopy(foreign(f), 1).wait_recv()

    def E(f, m):
        @pl.when(x > f)
        def _():
            landed(f, m)

    def L(f):
        @pl.when(x <= f)
        def _():
            for m in range(4):
                landed(f, m)

    def group(g):
        return pl.ds(g * GROUP, GROUP)

    def gain(b):
        return gains[b].astype(F32)

    def source(i, k):
        return pool[index_ref[k, 2 * x + i]]

    def weight(b):
        return lambda m: wts[b, m]

    def cs(b, m, g):
        def part(n, skip):
            product = dot(rows_of(n, 0, ROWS - skip), wts[b, m]).reshape(CLIPS, ROWS - skip, C)
            for k in range(CLIPS):
                at = pl.ds(g * GROUP + k * ROWS + skip, ROWS - skip)
                acc[at, :] = acc[at, :] + product[k]

        if m == 0 or m == 3:
            if b == 0:
                v = jnp.concatenate([source(g, k) for k in range(CLIPS)], axis=0)
            else:
                v = act[group(g), :]
        if m == 0:
            n = normalize(v, gain(b))
            nrm[group(g), :] = n
            acc[group(g), :] = dot(n, wts[b, 0])
        elif m < 3:
            part(nrm[group(g), :], m * SPATIAL)
        else:
            a = silu(acc[group(g), :]).astype(BF16)
            act[group(g), :] = (v.astype(F32) + dot(a, wts[b, 3])).astype(BF16)

    def cb(b, g):
        v = act[group(g), :]
        n = normalize(v, gain(b))
        a = silu(taps(n, weight(b))).astype(BF16)
        act[group(g), :] = (v.astype(F32) + dot(a, wts[b, 3])).astype(BF16)

    lane = lax.broadcasted_iota(jnp.int32, (8, 128), 1)
    row = lax.broadcasted_iota(jnp.int32, (8, 128), 0)

    def quantize(g):
        t = 4.0 * (dot_t(qwp[...], act[group(g), :]) + bias())
        codes = jnp.tanh(0.5 * t)
        back = lax.dot_general(
            codes.astype(BF16), pwp[...], (((0,), (0,)), ((), ())), preferred_element_type=F32
        )
        act[group(g), :] = back.astype(BF16)
        size = jnp.abs(t)
        e = jnp.exp(-size)
        entropy = jnp.log(1.0 + e) + size * e / (1.0 + e)
        bit = jnp.sum(0.5 * (1.0 + codes), axis=1, keepdims=True)
        ent = jnp.sum(entropy, axis=1, keepdims=True)
        at = lax.broadcasted_iota(jnp.int32, (PAD, 128), 0)
        col = lax.broadcasted_iota(jnp.int32, (PAD, 128), 1)
        bit = jnp.sum(jnp.where((at == col) & (col < BITS), bit, 0.0), axis=0, keepdims=True)
        ent = jnp.sum(jnp.where((at < BITS) & (col == BITS), ent, 0.0), axis=0, keepdims=True)
        return jnp.where(row == 2 * x + g, bit + ent, 0.0)

    def bias():
        at = lax.broadcasted_iota(jnp.int32, (PAD, 1), 0)
        value = jnp.zeros((PAD, 1), F32)
        for k in range(BITS):
            value = jnp.where(at == k, qb[k], value)
        return value

    def s1copy(dy, dz, sy, sz):
        k = dy * 4 + dz
        ref = stat1.at[sy * 4 + sz]
        return remote(ref, s1s.at[k], s1r.at[k], plane(dy, dz))

    def s2copy(d, e, sx, sc):
        k = d * 2 + e
        ref = stat2.at[sx * 2 + sc]
        return remote(ref, s2s.at[k], s2r.at[k], other(d, e))

    stored = [
        pltpu.make_async_copy(error_ref.at[g], error_hbm.at[g], osem.at[g]) for g in range(2)
    ] + [pltpu.make_async_copy(loss_ref, loss_hbm, osem.at[2])]

    def errors(g):
        for k in range(CLIPS):
            at = pl.ds(g * GROUP + k * ROWS, ROWS)
            differ = act[at, :].astype(F32) - source(g, k).astype(F32)
            square = differ * differ
            part = square[:, :128] + square[:, 128:256] + square[:, 256:384] + square[:, 384:]
            total = jnp.sum(part.T, axis=0, keepdims=True)
            error_ref[g, k : k + 1, :] = total * (1.0 / C)
        stored[g].start()

    def pool_ready():
        loads[3].wait()
        loads[4].wait()

    def quantizers():
        for load in loads[5:]:
            load.wait()
        qwp[...] = jnp.zeros_like(qwp)
        pwp[...] = jnp.zeros_like(pwp)
        qwp[0:BITS, :] = qw[...]
        pwp[0:BITS, :] = pw[...]

    def quantize_both():
        stat1[y * 4 + z] = quantize(0) + quantize(1)

    def s1send():
        for dy, dz in planes:
            s1copy(dy, dz, y, z).start()

    def s1take():
        for dy, dz in planes:
            s1copy(dy, dz, lax.rem(y + 4 - dy, 4), lax.rem(z + 4 - dz, 4)).wait_recv()
        total = stat1[0]
        for k in range(1, 16):
            total = total + stat1[k]
        stat2[x * 2 + c] = total

    def s2send():
        for d, e in others:
            s2copy(d, e, x, c).start()

    steps = {
        "X": X, "Y": Y, "V": V, "Z": Z, "R": R, "E": E, "L": L, "cs": cs, "cb": cb, "err": errors, "pool": pool_ready,
        "prep": quantizers, "quant": quantize_both, "s1send": s1send, "s1take": s1take, "s2send": s2send,
    }
    for name, *numbers in SCHEDULE:
        with jax.named_scope("_".join(map(str, [name, *numbers]))):
            steps[name](*numbers)

    with jax.named_scope("s2take"):
        for d, e in others:
            s2copy(d, e, lax.rem(x + 4 - d, 4), lax.rem(c + 2 - e, 2)).wait_recv()
    with jax.named_scope("loss"):
        total = stat2[0]
        for k in range(1, 8):
            total = total + stat2[k]
        mean = total / ROWS_TOTAL
        averaged = jnp.zeros((8, 128), F32)
        running = None
        for t in range(8):
            chosen = row == order_ref[t]
            marginal = jnp.sum(jnp.where(chosen, mean, 0.0), axis=0, keepdims=True)
            running = marginal if t == 0 else 0.5 * running + 0.5 * marginal
            averaged = jnp.where(chosen, running, averaged)
        smoothed = 0.05 + 0.9 * averaged
        smoothed = jnp.where(lane < BITS, smoothed, 0.5)
        terms = smoothed * jnp.log(smoothed) + (1.0 - smoothed) * jnp.log(1.0 - smoothed)
        terms = jnp.where(lane < BITS, terms, jnp.where(lane == BITS, mean, 0.0))
        loss = jnp.sum(terms, axis=1, keepdims=True)
        loss_ref[...] = jnp.sum(jnp.where(row == lane, loss, 0.0), axis=0, keepdims=True)

    stored[2].start()

    for d in (1, 3, 2):
        gcopy(x, d).wait_send()
    for m in range(4):
        xcopy(x, m, 1).wait_send()
        xcopy(x, m, 3).wait_send()
        if m in DIRECT:

            @pl.when(x == 0)
            def _():
                across(m).wait_send()

            @pl.when(x < 3)
            def _():
                relay(m).wait_send()
        else:
            relay(m).wait_send()
        for f in range(3):
            for d in (1, 3, 2):
                rcopy(foreign(f), m, d, q).wait_send()
            dcopy(foreign(f), m, c).wait_send()
    for dy, dz in planes:
        s1copy(dy, dz, y, z).wait_send()
    for d, e in others:
        s2copy(d, e, x, c).wait_send()
    for copy in stored:
        copy.wait()


def finish(error_in, loss_in, error_out, loss_out):
    error_out[...] = error_in[...]
    loss_out[...] = loss_in[:, 0:8]


def on_device(
    clip_pool, clip_index, batch_order, tap_weights, out_weights, norm_gains,
    quant_weight, quant_bias, post_weight,
):
    any_space = pl.BlockSpec(memory_space=pl.ANY)
    vmem = pl.BlockSpec(memory_space=pltpu.VMEM)
    dma = pltpu.SemaphoreType.DMA
    error, loss = pl.pallas_call(
        kernel,
        out_shape=(
            jax.ShapeDtypeStruct((2, CLIPS, ROWS), F32),
            jax.ShapeDtypeStruct((1, 128), F32),
        ),
        in_specs=[any_space] * 9,
        out_specs=(any_space, any_space),
        scratch_shapes=[
            pltpu.VMEM((32, ROWS, C), BF16),
            pltpu.VMEM((4, 4, C, C), BF16),
            pltpu.VMEM((4, 1, C), BF16),
            pltpu.VMEM((2 * GROUP, C), BF16),
            pltpu.VMEM((2 * GROUP, C), BF16),
            pltpu.VMEM((2 * GROUP, C), F32),
            pltpu.SMEM((CLIPS, 8), jnp.int32),
            pltpu.SMEM((8,), jnp.int32),
            pltpu.SMEM((BITS,), F32),
            pltpu.VMEM((BITS, C), BF16),
            pltpu.VMEM((BITS, C), BF16),
            pltpu.VMEM((PAD, C), BF16),
            pltpu.VMEM((PAD, C), BF16),
            pltpu.VMEM((16, 8, 128), F32),
            pltpu.VMEM((8, 8, 128), F32),
            pltpu.VMEM((2, CLIPS, ROWS), F32),
            pltpu.VMEM((1, 128), F32),
            dma((9,)),
            dma((3,)),
            dma((4, 2)),
            dma((4, 4)),
            dma((4,)),
            dma((4,)),
            dma((3,)),
            dma((4,)),
            dma((4, 4, 3)),
            dma((4, 4, 3)),
            dma((4, 4)),
            dma((4, 4)),
            dma((16,)),
            dma((16,)),
            dma((8,)),
            dma((8,)),
        ],
        compiler_params=pltpu.CompilerParams(
            collective_id=0, has_side_effects=True, vmem_limit_bytes=60 * 2**20
        ),
    )(
        clip_index.T, batch_order, clip_pool, tap_weights, out_weights, norm_gains,
        quant_weight.T, quant_bias, post_weight,
    )
    error, loss = pl.pallas_call(
        finish,
        out_shape=(
            jax.ShapeDtypeStruct((2, CLIPS, ROWS), F32),
            jax.ShapeDtypeStruct((1, 8), F32),
        ),
        in_specs=[vmem, vmem],
        out_specs=(vmem, vmem),
    )(error, loss)
    return error, loss.reshape(8)


def solution(mesh):
    torus = Mesh(
        mesh.devices.reshape(mesh.shape["section"], 4, 4, 2), ("section", "dp_0", "dp_1", "dp_2")
    )
    return jax.shard_map(
        on_device,
        mesh=torus,
        in_specs=(
            P(DP, None, None),
            P(None, DP),
            P(),
            P("section", None, None, None),
            P("section", None, None),
            P("section", None),
            P(),
            P(),
            P(),
        ),
        out_specs=(P("section", DP, None), P()),
        check_vma=False,
    )
```

time: 66.3 us -> 48.7 us (0.73)
  Pallas kernels: 57.4 us -> 47.9 us
  local copies, waits for them, and re-layouts: 5.97 us -> 0 us
  other arithmetic: 1.95 us -> 0 us
    pallas_call x1, Pallas kernels: 57.4 us -> 46.6 us  [on_device(): pl.pallas_call(kernel, out_shape=(jax.ShapeDtypeStruct((2, CLIPS, ROWS),...]
    unnamed x3 -> x0, local copies, waits for them, and re-layouts: 4.14 us -> none
    another operation x2 -> x0, other arithmetic: 1.95 us -> none
    slice x1 -> x0, local copies, waits for them, and re-layouts: 1.31 us -> none  [on_device(): return (error, loss[:, 0])]
    pallas_call x0 -> x1, Pallas kernels: none -> 1.3 us  [on_device(): pl.pallas_call(finish, out_shape=(jax.ShapeDtypeStruct((2, CLIPS, ROWS),...]
where the time goes in v2:
time: 48.7 us; the launch traced here: 48.6 us
  Pallas kernels  47.9 us (98%)
  between operations  0.64 us (1%)
    pallas_call x1, Pallas kernels, on_device(): pl.pallas_call(kernel, out_shape=(jax.ShapeDtypeStruct((2, CLIPS, ROWS),...  46.6 us
    pallas_call x1, Pallas kernels, on_device(): pl.pallas_call(finish, out_shape=(jax.ShapeDtypeStruct((2, CLIPS, ROWS),...  1.3 us

profile of v2, /device:TPU:1, one launch (start us, length us, event | category | flops | bytes accessed | tf_op | source)
XLA Modules:
  0.0 48.6 jit_solution(5507743206701778638)
XLA Ops:
  0.6 46.6 %shard_map.104 = (f32[2,4,256]{2,1,0:T(4,128)}, f32[1,128]{1,0:T(1,128)}) custom-call(s32[4,8]{1,0:T(4,128)} %bitcast.4, s32[8]{0:T(128)} %order_hbm.1, bf16[32,256,512]{2,1,0:T(8,128)(2,1)} %pool_hbm.1, bf16[1,3,512,512]{3,2,1,0:T(8,128)(2,1)} %taps_hbm.1, bf16[1,512,512]{2,1,0:T(8,128)(2,1)} %out_hbm.1, bf16[1,512]{1,0:T(2,128)(2,1)} %gains_hbm.1, ...), custom_call_target="tpu_custom_call" | custom-call | tf_op jit(solution)/shard_map/pallas_call | solution.py:458
  47.3 1.3 %shard_map.105 = (f32[2,4,256]{2,1,0:T(4,128)}, f32[1,8]{1,0:T(1,128)}) custom-call(f32[2,4,256]{2,1,0:T(4,128)} %get-tuple-element.6.error_in, f32[1,128]{1,0:T(1,128)} %get-tuple-element.7.loss_in), custom_call_target="tpu_custom_call" | custom-call | tf_op jit(solution)/shard_map/pallas_call | solution.py:508

commit v3 on v2

--- a/solution.py
+++ b/solution.py
@@ -22,20 +22,22 @@
 GROUP = CLIPS * ROWS
 NORM_EPS = 1e-06
 ROWS_TOTAL = 128.0 * 256.0
-DIRECT = (0, 2)
+DIRECT = (0, 1)
+LEFT = (2, 0, 3, 1)
 
 SCHEDULE = (
-    ("V", 0), ("X", 0, 0), ("Y", 0), ("V", 1), ("V", 2), ("X", 0, 1), ("Y", 1), ("V", 3), ("X", 0, 2),
-    ("Y", 2), ("X", 0, 3), ("Y", 3), ("R", 0, 0), ("X", 1, 0), ("X", 1, 1), ("Z", 0), ("Z", 1), ("R", 0, 1),
-    ("E", 0, 0), ("pool",), ("cs", 0, 0, 0), ("cs", 0, 0, 1), ("R", 0, 2), ("X", 1, 2), ("Z", 2), ("Z", 3),
-    ("E", 0, 1), ("cs", 0, 1, 0), ("cs", 0, 1, 1), ("R", 0, 3), ("X", 1, 3), ("E", 0, 2), ("cs", 0, 2, 0),
-    ("X", 2, 0), ("cs", 0, 2, 1), ("R", 1, 0), ("E", 0, 3), ("cs", 0, 3, 0), ("X", 2, 1), ("cs", 0, 3, 1),
-    ("prep",), ("R", 1, 1), ("X", 2, 2), ("L", 0), ("E", 1, 0), ("cs", 1, 0, 0), ("R", 1, 2), ("X", 2, 3),
-    ("cs", 1, 0, 1), ("E", 1, 1), ("cs", 1, 1, 0), ("R", 1, 3), ("cs", 1, 1, 1), ("E", 1, 2), ("cs", 1, 2, 0),
-    ("R", 2, 0), ("cs", 1, 2, 1), ("E", 1, 3), ("cs", 1, 3, 0), ("R", 2, 1), ("cs", 1, 3, 1), ("R", 2, 2),
-    ("quant",), ("s1send",), ("R", 2, 3), ("L", 1), ("E", 2, 0), ("E", 2, 1), ("E", 2, 2), ("E", 2, 3),
-    ("cb", 2, 0), ("cb", 2, 1), ("s1take",), ("s2send",), ("L", 2), ("cb", 3, 0), ("err", 0), ("cb", 3, 1),
-    ("err", 1),
+    ("T", 2), ("V", 0), ("X", 0, 0), ("Y", 0), ("V", 1), ("T", 3), ("X", 0, 1), ("Y", 1), ("V", 2),
+    ("X", 0, 2), ("Y", 2), ("V", 3), ("X", 0, 3), ("Y", 3), ("R", 0, 0), ("E", 0, 0), ("pool",),
+    ("cs", 0, 0, 0), ("W", 0), ("X", 1, 0), ("R", 0, 1), ("cs", 0, 0, 1), ("W", 1), ("X", 1, 1), ("Z", 0),
+    ("Z", 1), ("R", 0, 2), ("E", 0, 1), ("cs", 0, 1, 0), ("W", 2), ("X", 1, 2), ("cs", 0, 1, 1), ("X", 1, 3),
+    ("W", 3), ("Z", 2), ("Z", 3), ("R", 0, 3), ("E", 0, 2), ("cs", 0, 2, 0), ("S", 0), ("cs", 0, 2, 1),
+    ("R", 1, 0), ("E", 0, 3), ("cs", 0, 3, 0), ("X", 2, 0), ("X", 2, 1), ("cs", 0, 3, 1), ("R", 1, 1),
+    ("X", 2, 2), ("X", 2, 3), ("prep",), ("L", 0), ("E", 1, 0), ("cs", 1, 0, 0), ("R", 1, 2), ("cs", 1, 0, 1),
+    ("E", 1, 1), ("cs", 1, 1, 0), ("R", 1, 3), ("cs", 1, 1, 1), ("E", 1, 2), ("cs", 1, 2, 0), ("cs", 1, 2, 1),
+    ("S", 1), ("E", 1, 3), ("cs", 1, 3, 0), ("cs", 1, 3, 1), ("R", 2, 0), ("quant",), ("s1send",),
+    ("R", 2, 1), ("R", 2, 2), ("R", 2, 3), ("L", 1), ("E", 2, 0), ("E", 2, 1), ("E", 2, 2), ("ct", 2, 0),
+    ("S", 2), ("ct", 2, 1), ("E", 2, 3), ("co", 2, 0), ("co", 2, 1), ("s1take",), ("s2send",), ("L", 2),
+    ("cb", 3, 0), ("err", 0), ("cb", 3, 1), ("err", 1),
 )
 
 
@@ -81,7 +83,7 @@
     index_hbm, order_hbm, pool_hbm, taps_hbm, out_hbm, gains_hbm, qw_hbm, qb_hbm, pw_hbm,
     error_hbm, loss_hbm,
     pool, wts, gains, act, nrm, acc, index_ref, order_ref, qb, qw, pw, qwp, pwp, stat1, stat2, error_ref, loss_ref,
-    lsem, osem, xs, xr, ys, zs, gs, gr, rs, rr, ds, dr, s1s, s1r, s2s, s2r,
+    lsem, osem, xs, xr, wr, gs, gr, rs, rr, ds, dr, s1s, s1r, s2s, s2r,
 ):
     x = lax.axis_index("section")
     y = lax.axis_index("dp_0")
@@ -135,28 +137,37 @@
             ref, ref, send, recv, device_id=device, device_id_type=MESH
         )
 
+    def arrived(ref, semaphore):
+        pltpu.make_async_copy(ref, ref, semaphore).wait()
+
     def quarter(b, m, owner):
         return wts.at[b, m, pl.ds(pl.multiple_of(c * 256 + owner * 64, 64), 64)]
 
     def xcopy(b, m, d):
-        return remote(quarter(b, m, q), xs.at[m, d // 2], xr.at[b, m], xpeer(d))
+        return remote(quarter(b, m, q), xs, xr.at[b, m], xpeer(d))
 
     def relay(m):
         b = 3 - x
-        return remote(quarter(b, m, q), ys.at[m], xr.at[b, m], xpeer(1 + 2 * lax.rem(x, 2)))
+        return remote(quarter(b, m, q), xs, xr.at[b, m], xpeer(1 + 2 * lax.rem(x, 2)))
 
     def across(m):
-        return remote(quarter(0, m, q), zs.at[m], xr.at[0, m], xpeer(2))
+        return remote(quarter(0, m, q), xs, xr.at[0, m], xpeer(2))
+
+    def mate(m):
+        return lax.rem(q + (1 if m % 2 == 0 else 3) + 2 * lax.rem(q, 2), 4)
+
+    def second(m):
+        return remote(quarter(1, m, mate(m)), xs, wr.at[m], xpeer(1))
 
     def gcopy(b, d):
         return remote(gains.at[b], gs.at[d - 1], gr.at[b], xpeer(d))
 
     def rcopy(b, m, d, owner):
-        return remote(quarter(b, m, owner), rs.at[b, m, d - 1], rr.at[b, m, d - 1], ring(d))
+        return remote(quarter(b, m, owner), rs, rr.at[b, m], ring(d))
 
     def dcopy(b, m, h):
         ref = wts.at[b, m, pl.ds(pl.multiple_of(h * 256, 256), 256)]
-        return remote(ref, ds.at[b, m], dr.at[b, m], sibling)
+        return remote(ref, ds, dr.at[b, m], sibling)
 
     def foreign(f):
         return jnp.where(x <= f, f + 1, f)
@@ -169,7 +180,7 @@
         @pl.when(x == 0)
         def _():
             own(m, 1)
-            own(m, 3)
+            own(LEFT[m], 3)
             if m in DIRECT:
                 across(m).start()
 
@@ -186,11 +197,29 @@
         def _():
             own(m, 1)
 
+    @pl.when(x == 1)
+    def _():
+        for m in range(4):
+            second(m).start()
+
     for d in (1, 3, 2):
         gcopy(x, d).start()
 
     def take(f, m):
         xcopy(foreign(f), m, 1).wait_recv()
+
+    def pass_on(f, m):
+        for d in (1, 3, 2):
+            rcopy(foreign(f), m, d, q).start()
+
+    def W(m):
+        @pl.when(x == 2)
+        def _():
+            second(m).wait_recv()
+            there = mate(m + 1)
+            device = (x, there * (1 - c) + y * c, z * (1 - c) + there * c, c)
+            for at in (q, mate(m)):
+                remote(quarter(1, m, at), rs, rr.at[1, m], device).start()
 
     def V(m):
         @pl.when(x == 2)
@@ -207,6 +236,15 @@
             take(1, m)
             relay(m).start()
 
+    def T(m):
+        @pl.when(x == 3)
+        def _():
+            take(0, m)
+            relay(m).start()
+            if m == 3:
+                for k in range(4):
+                    own(k, 3)
+
     def Z(m):
         @pl.when(x == 0)
         def _():
@@ -215,15 +253,13 @@
 
     def X(f, m):
         if f == 0:
-            take(f, m)
-
-            @pl.when(x == 3)
-            def _():
-                if m not in DIRECT:
-                    relay(m).start()
-                if m == 3:
-                    for k in range(4):
-                        own(k, 3)
+            if m in DIRECT:
+                take(f, m)
+            else:
+
+                @pl.when(x < 3)
+                def _():
+                    take(f, m)
 
         elif f == 1:
 
@@ -236,13 +272,39 @@
             def _():
                 take(f, m)
 
-        for d in (1, 3, 2):
-            rcopy(foreign(f), m, d, q).start()
+        if f == 1:
+
+            @pl.when(x != 2)
+            def _():
+                pass_on(f, m)
+        else:
+            pass_on(f, m)
 
     def R(f, m):
-        for d in (1, 3, 2):
-            rcopy(foreign(f), m, d, lax.rem(q + 4 - d, 4)).wait_recv()
-        dcopy(foreign(f), m, c).start()
+        @pl.when(x > f)
+        def _():
+            gathered(f, m)
+
+    def S(f):
+        @pl.when(x <= f)
+        def _():
+            for m in range(4):
+                gathered(f, m)
+
+    def gathered(f, m):
+        b = foreign(f)
+        if f == 1:
+
+            @pl.when(x == 2)
+            def _():
+                arrived(wts.at[b, m, pl.ds(0, 128)], rr.at[b, m])
+
+            @pl.when(x != 2)
+            def _():
+                arrived(wts.at[b, m, pl.ds(0, 192)], rr.at[b, m])
+        else:
+            arrived(wts.at[b, m, pl.ds(0, 192)], rr.at[b, m])
+        dcopy(b, m, c).start()
 
     def landed(f, m):
         dcopy(foreign(f), m, 1 - c).wait_recv()
@@ -293,6 +355,14 @@
         else:
             a = silu(acc[group(g), :]).astype(BF16)
             act[group(g), :] = (v.astype(F32) + dot(a, wts[b, 3])).astype(BF16)
+
+    def ct(b, g):
+        n = normalize(act[group(g), :], gain(b))
+        nrm[group(g), :] = silu(taps(n, weight(b))).astype(BF16)
+
+    def co(b, g):
+        wide = act[group(g), :].astype(F32)
+        act[group(g), :] = (wide + dot(nrm[group(g), :], wts[b, 3])).astype(BF16)
 
     def cb(b, g):
         v = act[group(g), :]
@@ -329,14 +399,12 @@
         return value
 
     def s1copy(dy, dz, sy, sz):
-        k = dy * 4 + dz
         ref = stat1.at[sy * 4 + sz]
-        return remote(ref, s1s.at[k], s1r.at[k], plane(dy, dz))
+        return remote(ref, s1s, s1r, plane(dy, dz))
 
     def s2copy(d, e, sx, sc):
-        k = d * 2 + e
         ref = stat2.at[sx * 2 + sc]
-        return remote(ref, s2s.at[k], s2r.at[k], other(d, e))
+        return remote(ref, s2s, s2r, other(d, e))
 
     stored = [
         pltpu.make_async_copy(error_ref.at[g], error_hbm.at[g], osem.at[g]) for g in range(2)
@@ -372,8 +440,7 @@
             s1copy(dy, dz, y, z).start()
 
     def s1take():
-        for dy, dz in planes:
-            s1copy(dy, dz, lax.rem(y + 4 - dy, 4), lax.rem(z + 4 - dz, 4)).wait_recv()
+        arrived(stat1.at[pl.ds(0, 15)], s1r)
         total = stat1[0]
         for k in range(1, 16):
             total = total + stat1[k]
@@ -384,7 +451,7 @@
             s2copy(d, e, x, c).start()
 
     steps = {
-        "X": X, "Y": Y, "V": V, "Z": Z, "R": R, "E": E, "L": L, "cs": cs, "cb": cb, "err": errors, "pool": pool_ready,
+        "X": X, "T": T, "W": W, "S": S, "Y": Y, "V": V, "Z": Z, "R": R, "E": E, "L": L, "cs": cs, "ct": ct, "co": co, "cb": cb, "err": errors, "pool": pool_ready,
         "prep": quantizers, "quant": quantize_both, "s1send": s1send, "s1take": s1take, "s2send": s2send,
     }
     for name, *numbers in SCHEDULE:
@@ -392,8 +459,7 @@
             steps[name](*numbers)
 
     with jax.named_scope("s2take"):
-        for d, e in others:
-            s2copy(d, e, lax.rem(x + 4 - d, 4), lax.rem(c + 2 - e, 2)).wait_recv()
+        arrived(stat2.at[pl.ds(0, 7)], s2r)
     with jax.named_scope("loss"):
         total = stat2[0]
         for k in range(1, 8):
@@ -415,32 +481,30 @@
 
     stored[2].start()
 
-    for d in (1, 3, 2):
-        gcopy(x, d).wait_send()
-    for m in range(4):
-        xcopy(x, m, 1).wait_send()
-        xcopy(x, m, 3).wait_send()
-        if m in DIRECT:
-
-            @pl.when(x == 0)
-            def _():
-                across(m).wait_send()
-
-            @pl.when(x < 3)
-            def _():
-                relay(m).wait_send()
-        else:
-            relay(m).wait_send()
-        for f in range(3):
-            for d in (1, 3, 2):
-                rcopy(foreign(f), m, d, q).wait_send()
-            dcopy(foreign(f), m, c).wait_send()
-    for dy, dz in planes:
-        s1copy(dy, dz, y, z).wait_send()
-    for d, e in others:
-        s2copy(d, e, x, c).wait_send()
-    for copy in stored:
-        copy.wait()
+    with jax.named_scope("sent"):
+        for d in (1, 3, 2):
+            gcopy(x, d).wait_send()
+        arrived(wts.at[0, 0], xs)
+        for count, mine in ((384, x == 0), (512, x == 1), (256, x == 2), (128, x == 3)):
+
+            @pl.when(mine)
+            def _(count=count):
+                arrived(wts.at[0, 0, pl.ds(0, count)], xs)
+
+        for k in range(8):
+            arrived(wts.at[0, 0, pl.ds(0, 256)], rs)
+
+        @pl.when(x != 2)
+        def _():
+            arrived(wts.at[0, 0, pl.ds(0, 256)], rs)
+
+        for k in range(6):
+            arrived(wts.at[0, 0], ds)
+        arrived(stat1.at[pl.ds(0, 15)], s1s)
+        arrived(stat2.at[pl.ds(0, 7)], s2s)
+    with jax.named_scope("stored"):
+        for copy in stored:
+            copy.wait()
 
 
 def finish(error_in, loss_in, error_out, loss_out):
@@ -483,20 +547,19 @@
             pltpu.VMEM((1, 128), F32),
             dma((9,)),
             dma((3,)),
-            dma((4, 2)),
+            dma,
             dma((4, 4)),
-            dma((4,)),
             dma((4,)),
             dma((3,)),
             dma((4,)),
-            dma((4, 4, 3)),
-            dma((4, 4, 3)),
+            dma,
             dma((4, 4)),
+            dma,
             dma((4, 4)),
-            dma((16,)),
-            dma((16,)),
-            dma((8,)),
-            dma((8,)),
+            dma,
+            dma,
+            dma,
+            dma,
         ],
         compiler_params=pltpu.CompilerParams(
             collective_id=0, has_side_effects=True, vmem_limit_bytes=60 * 2**20

time: 48.7 us -> 46.1 us (0.947)
  Pallas kernels: 47.9 us -> 45.3 us
    pallas_call x1, Pallas kernels: 46.6 us -> 44 us  [on_device(): pl.pallas_call(kernel, out_shape=(jax.ShapeDtypeStruct((2, CLIPS, ROWS),...]
where the time goes in v3:
time: 46.1 us; the launch traced here: 45.9 us
  Pallas kernels  45.3 us (98%)
  between operations  0.64 us (1%)
    pallas_call x1, Pallas kernels, on_device(): pl.pallas_call(kernel, out_shape=(jax.ShapeDtypeStruct((2, CLIPS, ROWS),...  44 us
    pallas_call x1, Pallas kernels, on_device(): pl.pallas_call(finish, out_shape=(jax.ShapeDtypeStruct((2, CLIPS, ROWS),...  1.3 us

profile of v3, /device:TPU:1, one launch (start us, length us, event | category | flops | bytes accessed | tf_op | source)
XLA Modules:
  0.0 45.9 jit_solution(7907738250672573333)
XLA Ops:
  0.6 44.0 %shard_map.104 = (f32[2,4,256]{2,1,0:T(4,128)}, f32[1,128]{1,0:T(1,128)}) custom-call(s32[4,8]{1,0:T(4,128)} %bitcast.4, s32[8]{0:T(128)} %order_hbm.1, bf16[32,256,512]{2,1,0:T(8,128)(2,1)} %pool_hbm.1, bf16[1,3,512,512]{3,2,1,0:T(8,128)(2,1)} %taps_hbm.1, bf16[1,512,512]{2,1,0:T(8,128)(2,1)} %out_hbm.1, bf16[1,512]{1,0:T(2,128)(2,1)} %gains_hbm.1, ...), custom_call_target="tpu_custom_call" | custom-call | tf_op jit(solution)/shard_map/pallas_call | solution.py:522
  44.6 1.3 %shard_map.105 = (f32[2,4,256]{2,1,0:T(4,128)}, f32[1,8]{1,0:T(1,128)}) custom-call(f32[2,4,256]{2,1,0:T(4,128)} %get-tuple-element.6.error_in, f32[1,128]{1,0:T(1,128)} %get-tuple-element.7.loss_in), custom_call_target="tpu_custom_call" | custom-call | tf_op jit(solution)/shard_map/pallas_call | solution.py:571
